TPU v7x, 32 devices: a whole 2x2x4 slice. The times are simulated.
32 devices in a mesh: coil: 8 (over y, x, core), kz: 4 (over z).
Axes of the slice: x: 2, y: 2, z: 4, core: 2. Of those that a mesh axis runs over, the one named last changes fastest.
Arguments:
- kdata: bfloat16 [2, 64, 8, 256, 512], P(None, 'kz', 'coil'), may hold values from -6 to 6
- spoke_angle: int32 [256], replicated, may hold values from 0 to 63
- spoke_count: int32 [64], P('kz'), may hold values from 128 to 256
- block_index: int32 [64, 4], replicated, may hold values from 0 to 511
- interp: bfloat16 [64, 4, 128, 128], replicated, may hold values from -0.5 to 0.5
- sens_maps: bfloat16 [2, 8, 256, 256], P(None, 'coil'), may hold values from -5 to 5
Outputs:
- image: float32 [2, 64, 256, 256], P(None, 'kz', 'coil')
Inputs may be any that keep to these rules, and one draw needn't show every extreme that they name: Partition p uses its first spoke_count[p] spokes. `block_index`: several segments may hit the same grid block.
All inputs are finite; a program needn't handle non-finite values.
Results may differ from a plain program's by a relative error of at most 0.0059.
Values sent between devices are 32-bit elements; how exact they have to be, the bound alone decides.
A program may use at most 128 MiB of HBM per device.

v0:
```python
import jax
import jax.numpy as jnp
from jax import lax
from jax.sharding import PartitionSpec as P


def dft_tables(length, dtype):
    index = jnp.arange(length, dtype=jnp.int32)
    product = index[:, None] * index[None, :] % length
    phase = product.astype(jnp.float32) * (2.0 * jnp.pi / length)
    scale = 1.0 / jnp.sqrt(jnp.float32(length))
    return ((jnp.cos(phase) * scale).astype(dtype), (jnp.sin(phase) * scale).astype(dtype))


def kz_block(z_first, z_count, k_count, length):
    z_index = z_first + jnp.arange(z_count, dtype=jnp.int32)
    k_index = jnp.arange(k_count, dtype=jnp.int32)
    product = z_index[:, None] * k_index[None, :] % length
    phase = product.astype(jnp.float32) * (2.0 * jnp.pi / length)
    scale = 1.0 / jnp.sqrt(jnp.float32(length))
    return (jnp.cos(phase) * scale, jnp.sin(phase) * scale)


def kz_apply(cos_z, sin_z, slab):
    high = lax.Precision.HIGHEST
    real_part = jnp.einsum("zk,kyx->zyx", cos_z, slab[0], precision=high) + jnp.einsum(
        "zk,kyx->zyx", sin_z, slab[1], precision=high
    )
    imag_part = jnp.einsum("zk,kyx->zyx", cos_z, slab[1], precision=high) - jnp.einsum(
        "zk,kyx->zyx", sin_z, slab[0], precision=high
    )
    return jnp.stack([real_part, imag_part])


def coil_image(data, weights, interp, block_index, cos_t, sin_t):
    f32 = jnp.float32
    binned = jnp.einsum("rpsn,psa->rpan", data, weights, preferred_element_type=f32).astype(
        jnp.bfloat16
    )
    rdim, pdim, adim, mdim = binned.shape
    seg = interp.shape[2]
    gdim = mdim // seg
    side = cos_t.shape[0]
    pieces = binned.reshape(rdim, pdim, adim, gdim, seg)
    contrib = jnp.einsum("rpagj,agjt->rpagt", pieces, interp, preferred_element_type=f32)
    flat = jnp.zeros((rdim, pdim, side * side // seg, seg), f32)
    flat = flat.at[:, :, block_index.reshape(-1)].add(contrib.reshape(rdim, pdim, adim * gdim, seg))
    grid = flat.reshape(rdim, pdim, side, side).astype(jnp.bfloat16)
    half_re = jnp.einsum("ky,pyx->pkx", cos_t, grid[0], preferred_element_type=f32) + jnp.einsum(
        "ky,pyx->pkx", sin_t, grid[1], preferred_element_type=f32
    )
    half_im = jnp.einsum("ky,pyx->pkx", cos_t, grid[1], preferred_element_type=f32) - jnp.einsum(
        "ky,pyx->pkx", sin_t, grid[0], preferred_element_type=f32
    )
    half_re = half_re.astype(jnp.bfloat16)
    half_im = half_im.astype(jnp.bfloat16)
    out_re = jnp.einsum("pkx,mx->pkm", half_re, cos_t, preferred_element_type=f32) + jnp.einsum(
        "pkx,mx->pkm", half_im, sin_t, preferred_element_type=f32
    )
    out_im = jnp.einsum("pkx,mx->pkm", half_im, cos_t, preferred_element_type=f32) - jnp.einsum(
        "pkx,mx->pkm", half_re, sin_t, preferred_element_type=f32
    )
    return jnp.stack([out_re, out_im])


def conj_product(sens, image):
    real_part = sens[0] * image[0] + sens[1] * image[1]
    imag_part = sens[0] * image[1] - sens[1] * image[0]
    return jnp.stack([real_part, imag_part])


def per_device(kdata, spoke_angle, spoke_count, block_index, interp, sens_maps):
    side = sens_maps.shape[2]
    parts_here = kdata.shape[1]
    spokes = kdata.shape[3]
    angles = interp.shape[0]
    cos_t, sin_t = dft_tables(side, jnp.bfloat16)
    position = jnp.arange(spokes, dtype=jnp.int32)
    used = position[None, :] < spoke_count[:, None]
    match = spoke_angle[:, None] == jnp.arange(angles, dtype=jnp.int32)[None, :]
    weights = (used[:, :, None] & match[None, :, :]).astype(jnp.bfloat16)
    data = kdata[:, :, 0]
    image_c = coil_image(data, weights, interp, block_index, cos_t, sin_t)
    sens_here = sens_maps.astype(jnp.float32)
    weighted = conj_product(sens_here[:, 0][:, None], image_c)
    combined = lax.psum_scatter(weighted, "coil", scatter_dimension=2, tiled=True)
    groups = lax.axis_size("kz")
    kz_total = parts_here * groups
    my_first = lax.axis_index("kz") * parts_here
    piece = lax.all_gather(combined, "kz", axis=1, tiled=True)
    cos_z, sin_z = kz_block(my_first, parts_here, piece.shape[1], kz_total)
    return kz_apply(cos_z, sin_z, piece)


def solution(mesh):
    placed = (
        P(None, "kz", "coil", None, None),
        P(),
        P("kz"),
        P(),
        P(),
        P(None, "coil", None, None),
    )
    return jax.shard_map(
        per_device,
        mesh=mesh,
        in_specs=placed,
        out_specs=P(None, "kz", "coil", None),
        check_vma=False,
    )
```

profile of v0, /device:TPU:0, one launch (start us, length us, event | category | flops | bytes accessed | tf_op | source)
XLA Modules:
  0.0 278.5 jit_solution(6729629359910109795)
XLA Ops:
  6.5 0.0 reduce-scatter.2.cloned.1.call-start
  6.5 0.7 iota_compare_fusion
  7.2 0.7 iota_compare_fusion.1
  8.0 6.2 %convert_bitcast_fusion = bf16[2,16,64,512]{3,2,0,1:T(8,128)(2,1)} fusion(pred[256,64]{0,1:T(8,128)(4,1)S(1)} %iota_compare_fusion, pred[16,256]{1,0:T(8,128)(4,1)S(1)} %iota_compare_fusion.1, bf16[2,16,1,256,512]{4,3,2,1,0:T(8,128)(2,1)} %param.6), kind=kOutput, calls=%fused_computation.21 | convolution fusion | flops 538181632 | bytes 10506240 | tf_op jit(solution)/shard_map/rpsn,psa->rpan/dot_general | solution.py:37
  14.2 0.0 copy-start.4
  14.2 2.6 reshape.89
  16.7 0.0 copy-done.4
  16.7 0.1 copy.18
  16.8 0.1 reshape.88
  17.0 7.7 %fusion = f32[64,4,2,16,128]{4,3,2,1,0:T(8,128)} fusion(bf16[64,4,128,128]{3,2,1,0:T(8,128)(2,1)} %param.10, bf16[2,16,64,4,128]{4,3,2,0,1:T(4,128)(2,1)S(1)} %reshape.89), kind=kOutput, calls=%fused_computation.2 | convolution fusion | flops 268435456 | bytes 14680064 | tf_op jit(solution)/shard_map/rpagj,agjt->rpagt/dot_general | solution.py:45
  24.6 3.8 %broadcast_in_dim.2 = f32[2,16,512,128]{3,1,2,0:T(8,128)} broadcast(f32[]{:T(128)} %constant.42.clone.1), dimensions={} | broadcast | bytes 8388612 | tf_op jit(solution)/shard_map/broadcast_in_dim | solution.py:46
  28.4 34.5 %scatter_fusion = f32[2,16,512,128]{3,1,2,0:T(8,128)} fusion(f32[2,16,512,128]{3,1,2,0:T(8,128)} %broadcast_in_dim.2, s32[256]{0:T(256)S(1)} %bitcast.87, f32[256,2,16,128]{3,2,1,0:T(8,128)} %bitcast.86), kind=kCustom, calls=%fused_computation | custom fusion | flops 1048576 | bytes 12583936 | tf_op jit(solution)/shard_map/scatter-add | solution.py:47
  62.9 3.9 %convert_element_type.68 = bf16[2,16,512,128]{3,1,2,0:T(8,128)(2,1)S(1)} convert(f32[2,16,512,128]{3,1,2,0:T(8,128)} %scatter_fusion) | non-fusion elementwise | flops 2097152 | bytes 12582912 | tf_op jit(solution)/shard_map/convert_element_type | solution.py:48
  66.9 2.0 fusion.133
  68.9 1.9 copy.21
  70.8 2.7 squeeze.11
  73.5 0.0 copy-start.2
  73.5 3.6 %fusion.53 = f32[16,256,256]{2,1,0:T(8,128)} fusion(bf16[16,256,256]{2,1,0:T(8,128)(2,1)S(1)} %squeeze.11), kind=kOutput, calls=%fused_computation.55 | convolution fusion | flops 537919488 | bytes 6291456 | tf_op jit(solution)/shard_map/ky,pyx->pkx/dot_general | solution.py:49
  77.1 0.0 copy-done.2
  77.1 1.9 copy.23
  78.9 4.1 %squeeze.12 = bf16[16,256,256]{2,1,0:T(8,128)(2,1)} reshape(bf16[1,16,512,128]{3,2,1,0:T(8,128)(2,1)} %copy.23) | data formatting | bytes 4194304 | tf_op jit(solution)/shard_map/squeeze | solution.py:50
  83.1 0.0 copy-start
  83.1 0.0 copy-start.1
  83.1 3.4 %fusion.50 = f32[16,256,256]{2,1,0:T(8,128)S(1)} fusion(bf16[16,256,256]{2,1,0:T(8,128)(2,1)} %squeeze.12), kind=kOutput, calls=%fused_computation.54 | convolution fusion | flops 537919488 | bytes 6291456 | tf_op jit(solution)/shard_map/ky,pyx->pkx/dot_general | solution.py:52
  86.5 0.0 copy-done
  86.5 0.0 copy-done.1
  86.5 1.7 add_convert_fusion
  88.2 1.7 subtract_convert_fusion
  89.9 1.7 fusion.4
  91.6 1.7 fusion.8
  93.3 0.0 copy-start.3
  93.3 1.7 convolution_subtract_fusion
  95.0 0.0 copy-done.3
  95.1 2.7 add_bitcast_fusion
  97.8 3.8 %pad_maximum_fusion = f32[2,16,256,256]{3,2,1,0:T(8,128)} fusion(f32[1,16,256,256]{3,2,1,0:T(8,128)S(1)} %get-tuple-element.6, f32[1,16,256,256]{3,2,1,0:T(8,128)S(1)} %get-tuple-element.5), kind=kLoop, calls=%fused_computation.1 | loop fusion | flops 2097152 | bytes 16777216 | tf_op jit(solution)/shard_map/stack | solution.py:69
  101.6 0.0 reduce-scatter.2.cloned.1.call-update
  101.6 0.0 all-gather.2.cloned.1.call-start
  101.7 74.3 %reduce-scatter.2.cloned.1.call-done = f32[2,16,32,256]{3,2,1,0:T(8,128)} async-done(((f32[2,16,256,256]{3,2,1,0:T(8,128)}), f32[2,16,32,256]{3,2,1,0:T(8,128)}) %reduce-scatter.2.cloned.1.call-update) | async-done | bytes 1048592 | tf_op jit(solution)/shard_map/reduce_scatter | solution.py:86
  175.9 0.0 all-gather.2.cloned.1.call-update
  176.0 82.3 %all-gather.2.cloned.1.call-done = f32[2,64,32,256]{3,2,1,0:T(8,128)} async-done(((f32[2,16,32,256]{3,2,1,0:T(8,128)}), f32[2,64,32,256]{3,2,1,0:T(8,128)}) %all-gather.2.cloned.1.call-update) | async-done | bytes 4194320 | tf_op jit(solution)/shard_map/all_gather | solution.py:90
  258.3 2.5 slice_bitcast_fusion.1
  260.8 2.3 fusion.13
  263.1 2.3 fusion.11
  265.4 2.3 fusion.24
  267.7 2.3 fusion.30
  270.0 0.1 pad_maximum_fusion.1
  270.1 1.6 copy.35
  (4 shorter events, 0.1 us)
Async XLA Ops:
  6.5 169.4 %reduce-scatter.2.cloned.1.call-start = ((), (), s32[]{:S(2)}) async-start(), calls=%async_computation.1 | async-start | bytes 9437184 | tf_op jit(solution)/shard_map/reduce_scatter | solution.py:86
  14.2 2.6 copy-start.4
  73.5 3.6 %copy-start.2 = (bf16[1,16,512,128]{3,1,2,0:T(8,128)(2,1)S(1)}, bf16[1,16,512,128]{3,1,2,0:T(8,128)(2,1)}, u32[]{:S(2)}) copy-start(bf16[1,16,512,128]{3,1,2,0:T(8,128)(2,1)} %get-tuple-element.9) | copy-start | bytes 6291460
  83.1 3.4 %copy-start = (bf16[16,256,256]{2,1,0:T(8,128)(2,1)S(1)}, bf16[16,256,256]{2,1,0:T(8,128)(2,1)}, u32[]{:S(2)}) copy-start(bf16[16,256,256]{2,1,0:T(8,128)(2,1)} %squeeze.12) | copy-start | bytes 6291460
  83.1 3.5 %copy-start.1 = (f32[16,256,256]{2,1,0:T(8,128)S(1)}, f32[16,256,256]{2,1,0:T(8,128)}, u32[]{:S(2)}) copy-start(f32[16,256,256]{2,1,0:T(8,128)} %fusion.53) | copy-start | bytes 12582916
  93.3 1.7 copy-start.3
  101.6 156.6 %all-gather.2.cloned.1.call-start = ((), (), s32[]{:S(2)}) async-start(), calls=%async_computation.2 | async-start | bytes 5242880 | tf_op jit(solution)/shard_map/all_gather | solution.py:90
Sparse Core Ops, SparseCore 0:
  101.7 74.1 reduce-scatter.1
  177.5 80.7 all-gather.1
where the time goes:
time: 279 us
  waiting for transfers between devices  157 us (56%)
  other arithmetic  43.8 us (16%)
  matrix products  41.2 us (15%)
  local copies, waits for them, and re-layouts  23.3 us (8%)
  between operations  13.6 us (5%)
    all_gather x1, waiting for transfers between devices, per_device(): piece = lax.all_gather(combined, 'kz', axis=1, tiled=True)  82.3 us
    reduce_scatter x1, waiting for transfers between devices, per_device(): lax.psum_scatter(weighted, 'coil', scatter_dimension=2, tiled=True)  74.3 us
    scatter-add x1, other arithmetic, coil_image(): flat.at[:, :, block_index.reshape(-1)]  34.5 us
    dot_general x1, matrix products, coil_image(): jnp.einsum('rpagj,agjt->rpagt', pieces, interp, preferred_element_type=f32)  7.66 us
    dot_general x1, matrix products, coil_image(): jnp.einsum('rpsn,psa->rpan', data, weights, preferred_element_type=f32)  6.2 us
  transfers between devices with their start and end apart: 2, of which 2 were waited for; matrix products, arithmetic and copies ran while one was open for 0% of the time, Pallas kernels for 0%

commit v1 on v0

v1 whole, which is shorter than its diff:
```python
import functools
import math

import jax
import jax.numpy as jnp
from jax import lax
from jax.experimental import pallas as pl
from jax.experimental.pallas import tpu as pltpu
from jax.sharding import PartitionSpec as P

F32 = jnp.float32
BF16 = jnp.bfloat16
SUB = 2


def cos_sin(product, length, dtype):
    phase = (product % length).astype(F32) * (2.0 * jnp.pi / length)
    scale = 1.0 / jnp.sqrt(F32(length))
    return ((jnp.cos(phase) * scale).astype(dtype), (jnp.sin(phase) * scale).astype(dtype))


def halving_orders(bits):
    first = list(range(bits))
    return [first, first[:1] + first[:0:-1]]


def kernel(bits, groups, parts, rows, side, *refs):
    contrib, ymat, xmat, sens, twiddle, out = refs[:6]
    weighted, gathered = refs[6:8]
    inbox = refs[8 : 8 + bits]
    half_send, half_recv, ring_send, ring_recv = refs[8 + bits :]
    blocks = 1 << bits
    orders = halving_orders(bits)
    steps = parts // SUB
    coil = lax.axis_index("coil")
    kz = lax.axis_index("kz")
    my_bit = [(coil // (1 << bit)) % 2 for bit in range(bits)]
    partner = [coil + (1 - 2 * my_bit[bit]) * (1 << bit) for bit in range(bits)]
    right = (kz + 1) % groups
    left = (kz + groups - 1) % groups

    barrier = pltpu.get_barrier_semaphore()
    for bit in range(bits):
        pl.semaphore_signal(barrier, 1, device_id={"coil": partner[bit]})
    pl.semaphore_signal(barrier, 1, device_id={"kz": right})
    pl.semaphore_signal(barrier, 1, device_id={"kz": left})
    pl.semaphore_wait(barrier, bits + 2)

    def kept_start(order, stage):
        start = 0
        for s in range(stage):
            start = start + my_bit[order[s]] * (blocks >> (s + 1))
        return start

    def half_copy(part, sub, stage):
        order = orders[sub % 2]
        bit = order[stage]
        size = blocks >> (stage + 1)
        start = kept_start(order, stage) + (1 - my_bit[bit]) * size
        return pltpu.make_async_remote_copy(
            src_ref=weighted.at[part, pl.ds(start, size)],
            dst_ref=inbox[stage].at[part],
            send_sem=half_send.at[stage, part],
            recv_sem=half_recv.at[stage, part],
            device_id={"coil": partner[bit]},
        )

    def add_inbox(part, sub, stage):
        size = blocks >> (stage + 1)
        start = kept_start(orders[sub % 2], stage + 1)
        total = weighted[part, pl.ds(start, size)] + inbox[stage][part]
        if stage < bits - 1:
            weighted[part, pl.ds(start, size)] = total
        else:
            gathered[part, 0] = total[0]

    far = groups // 2

    def ring_copies(part, hop):
        copies = []
        for way in range(2):
            if way == 0:
                source, target, to = hop - 1, hop, right
            else:
                source, target, to = (groups - hop + 1) % groups, groups - hop, left
            if hop == far:
                src, dst = gathered.at[part, source, way], gathered.at[part, target, way]
            else:
                src, dst = gathered.at[part, source], gathered.at[part, target]
            copies.append(
                pltpu.make_async_remote_copy(
                    src_ref=src,
                    dst_ref=dst,
                    send_sem=ring_send.at[hop - 1, way, part],
                    recv_sem=ring_recv.at[hop - 1, way, part],
                    device_id={"kz": to},
                )
            )
        return copies

    def compute(step):
        first = step * SUB
        data = jnp.concatenate([contrib[first + s] for s in range(SUB)], axis=1)
        seg = data.shape[1] // SUB
        halves = [
            jnp.dot(ymat[h], data, preferred_element_type=F32).astype(BF16)
            for h in range(side // seg)
        ]
        s_re = sens[0].astype(F32)
        s_im = sens[1].astype(F32)
        for s in range(SUB):
            pieces = [h[r * side : (r + 1) * side, s * seg : (s + 1) * seg] for r in range(2) for h in halves]
            image = jnp.dot(jnp.concatenate(pieces, axis=1), xmat[...], preferred_element_type=F32)
            i_re, i_im = image[:, :side], image[:, side:]
            result = [s_re * i_re + s_im * i_im, s_re * i_im - s_im * i_re]
            order = orders[s % 2]
            for block in range(blocks):
                place = 0
                for bit in order:
                    place = place * 2 + (block >> bit) % 2
                for r in range(2):
                    weighted[first + s, place, r] = result[r][block * rows : (block + 1) * rows]

    def transform(step):
        group = 8
        for row in range(0, rows, group):
            inner = []
            for s in range(SUB):
                x = [[gathered[step * SUB + s, j, r, row : row + group] for r in range(2)] for j in range(groups)]
                per_q = []
                for q in range(groups):
                    re = im = None
                    for j in range(groups):
                        angle = 2.0 * math.pi * (q * j % groups) / groups
                        c, d = round(math.cos(angle), 12), round(math.sin(angle), 12)
                        for coef, a, b in ((c, x[j][0], x[j][1]), (d, -x[j][1], x[j][0])):
                            if coef == 0.0:
                                continue
                            ta = a if coef == 1.0 else a * F32(coef)
                            tb = b if coef == 1.0 else b * F32(coef)
                            re = ta if re is None else re + ta
                            im = tb if im is None else im + tb
                    per_q.append((re, im))
                inner.append(per_q)
            for z in range(parts):
                a_re = out[0, z, row : row + group]
                a_im = out[1, z, row : row + group]
                for s in range(SUB):
                    k = step * SUB + s
                    c, d = twiddle[0, k, z], twiddle[1, k, z]
                    re, im = inner[s][z % groups]
                    a_re = a_re + (c * re + d * im)
                    a_im = a_im + (c * im - d * re)
                out[0, z, row : row + group] = a_re
                out[1, z, row : row + group] = a_im

    out[...] = jnp.zeros_like(out)
    lags = [0, 1]
    for _ in range(bits + far - 1):
        lags.append(lags[-1] + 2)

    def tick(t, carry):
        def at(index, body):
            step = t - lags[index]

            @pl.when((step >= 0) & (step < steps))
            def _():
                body(step)

        def begin(step):
            compute(step)
            for s in range(SUB):
                half_copy(step * SUB + s, s, 0).start()

        at(0, begin)
        for stage in range(bits):

            def reduce_stage(step, stage=stage):
                for s in range(SUB):
                    part = step * SUB + s
                    half_copy(part, s, stage).wait_recv()
                    add_inbox(part, s, stage)
                    if stage < bits - 1:
                        half_copy(part, s, stage + 1).start()
                    else:
                        for copy in ring_copies(part, 1):
                            copy.start()

            at(1 + stage, reduce_stage)
        for hop in range(1, far + 1):

            def ring_stage(step, hop=hop):
                for s in range(SUB):
                    part = step * SUB + s
                    for copy in ring_copies(part, hop):
                        copy.wait_recv()
                    if hop < far:
                        for copy in ring_copies(part, hop + 1):
                            copy.start()
                if hop == far:
                    transform(step)

            at(bits + hop, ring_stage)
        return carry

    lax.fori_loop(0, steps + lags[-1], tick, 0)

    def finish(step, carry):
        for s in range(SUB):
            part = step * SUB + s
            for stage in range(bits):
                half_copy(part, s, stage).wait_send()
            for hop in range(1, far + 1):
                for copy in ring_copies(part, hop):
                    copy.wait_send()
        return carry

    lax.fori_loop(0, steps, finish, 0)


def per_device(kdata, spoke_angle, spoke_count, block_index, interp, sens_maps):
    side = sens_maps.shape[2]
    parts = kdata.shape[1]
    spokes = kdata.shape[3]
    angles, segs, seg = interp.shape[:3]
    coils = lax.axis_size("coil")
    groups = lax.axis_size("kz")
    bits = coils.bit_length() - 1
    rows = side // coils
    length = parts * groups
    kz = lax.axis_index("kz")

    position = jnp.arange(spokes, dtype=jnp.int32)
    used = position[None, :] < spoke_count[:, None]
    match = spoke_angle[:, None] == jnp.arange(angles, dtype=jnp.int32)[None, :]
    weights = (used[:, :, None] & match[None, :, :]).astype(BF16)
    binned = jnp.einsum("rpsn,psa->rpan", kdata[:, :, 0], weights, preferred_element_type=F32).astype(BF16)
    pieces = binned.reshape(2, parts, angles, segs, seg)
    contrib = jnp.einsum("rpagj,agjt->pragt", pieces, interp, preferred_element_type=F32).astype(BF16)
    hits = angles * segs
    contrib = contrib.reshape(parts, 2 * hits, seg)

    across = side // seg
    index = jnp.arange(side, dtype=jnp.int32)
    where = block_index.reshape(-1)
    hit_y = where // across
    hit_x = where % across
    cos_y, sin_y = cos_sin(index[:, None] * hit_y[None, :], side, F32)
    here = (jnp.arange(across, dtype=jnp.int32)[:, None, None] == hit_x).astype(F32)
    cos_y, sin_y = cos_y * here, sin_y * here
    ymat = jnp.concatenate(
        [jnp.concatenate([cos_y, sin_y], 2), jnp.concatenate([-sin_y, cos_y], 2)], 1
    ).astype(BF16)
    cos_x, sin_x = cos_sin(index[:, None] * index[None, :], side, F32)
    xmat = jnp.concatenate(
        [jnp.concatenate([cos_x, -sin_x], 1), jnp.concatenate([sin_x, cos_x], 1)], 0
    ).astype(BF16)
    mine = kz * parts + jnp.arange(parts, dtype=jnp.int32)
    twiddle = jnp.stack(cos_sin(mine[:, None] * mine[None, :], length, F32))

    block = (2, rows, side)
    vmem = pl.BlockSpec(memory_space=pltpu.VMEM)
    far = groups // 2
    scratch = [
        pltpu.VMEM((parts, coils) + block, F32),
        pltpu.VMEM((parts, groups) + block, F32),
    ]
    scratch += [pltpu.VMEM((parts, coils >> (s + 1)) + block, F32) for s in range(bits)]
    scratch += [pltpu.SemaphoreType.DMA((bits, parts))] * 2
    scratch += [pltpu.SemaphoreType.DMA((far, 2, parts))] * 2
    return pl.pallas_call(
        functools.partial(kernel, bits, groups, parts, rows, side),
        out_shape=jax.ShapeDtypeStruct((2, parts, rows, side), F32),
        in_specs=[vmem] * 4 + [pl.BlockSpec(memory_space=pltpu.SMEM)],
        out_specs=vmem,
        scratch_shapes=scratch,
        compiler_params=pltpu.CompilerParams(
            collective_id=0, has_side_effects=True, vmem_limit_bytes=60 * 1024 * 1024
        ),
        name="combine",
    )(contrib, ymat, xmat, sens_maps[:, 0], twiddle)


def solution(mesh):
    placed = (
        P(None, "kz", "coil", None, None),
        P(),
        P("kz"),
        P(),
        P(),
        P(None, "coil", None, None),
    )
    return jax.shard_map(
        per_device,
        mesh=mesh,
        in_specs=placed,
        out_specs=P(None, "kz", "coil", None),
        check_vma=False,
    )
```

time: 279 us -> 121 us (0.43)
  waiting for transfers between devices: 157 us -> 0 us
  Pallas kernels: 0 us -> 95.6 us
  other arithmetic: 43.8 us -> 7.3 us
  matrix products: 41.2 us -> 11.2 us
  local copies, waits for them, and re-layouts: 23.3 us -> 7.02 us
  between operations: 13.6 us -> 0.07 us
    pallas_call x0 -> x1, Pallas kernels: none -> 95.6 us  [per_device(): pl.pallas_call(functools.partial(kernel, bits, groups, parts, rows, side)...]
    all_gather x1 -> x0, waiting for transfers between devices: 82.3 us -> none  [per_device(): piece = lax.all_gather(combined, 'kz', axis=1, tiled=True)]
    reduce_scatter x1 -> x0, waiting for transfers between devices: 74.3 us -> none  [per_device(): lax.psum_scatter(weighted, 'coil', scatter_dimension=2, tiled=True)]
    scatter-add x1 -> x0, other arithmetic: 34.5 us -> none  [coil_image(): flat.at[:, :, block_index.reshape(-1)]]
    dot_general x14 -> x2, matrix products: 41.2 us -> 11.2 us  [the longest x1 6.31 us: per_device(): jnp.einsum('rpagj,agjt->pragt', pieces, interp, preferred_element_type=F32)]
    squeeze x3 -> x0, local copies, waits for them, and re-layouts: 9.34 us -> none  [the longest x1 4.13 us: coil_image(): grid[1]]
    slice x3 -> x0, local copies, waits for them, and re-layouts: 5.78 us -> none  [the longest x2 3.9 us: coil_image(): grid[1]]
    convert_element_type x2 -> x1, other arithmetic: 3.96 us -> 0.01 us  [per_device(): (jnp.arange(across, dtype=jnp.int32)[:, None, None] == hit_x).astype(F32)]
  transfers between devices with their start and end apart: 2 -> 0, of which waited for: 2 -> 0; matrix products, arithmetic and copies ran while one was open for 0% -> 0% of each run, Pallas kernels for 0% -> 0%
where the time goes in v1:
time: 121 us
  Pallas kernels  95.6 us (79%)
  matrix products  11.2 us (9%)
  other arithmetic  7.3 us (6%)
  local copies, waits for them, and re-layouts  7.02 us (6%)
    pallas_call x1, Pallas kernels, per_device(): pl.pallas_call(functools.partial(kernel, bits, groups, parts, rows, side)...  95.6 us
    dot_general x1, matrix products, per_device(): jnp.einsum('rpagj,agjt->pragt', pieces, interp, preferred_element_type=F32)  6.31 us
    dot_general x1, matrix products, per_device(): jnp.einsum('rpsn,psa->rpan', kdata[:, :, 0], weights, preferred_element_t...  4.86 us
    convert_element_type x1, local copies, waits for them, and re-layouts, per_device(): jnp.einsum('rpagj,agjt->pragt', pieces, interp, preferred_element_type=F32)  2.43 us

profile of v1, /device:TPU:0, one launch (start us, length us, event | category | flops | bytes accessed | tf_op | source)
XLA Modules:
  0.0 121.1 jit_solution(5736550766780185083)
XLA Ops:
  0.0 0.7 iota_compare_fusion
  0.7 0.7 iota_compare_fusion.1
  1.4 4.9 %convert_bitcast_fusion.1 = bf16[2,16,64,512]{3,2,0,1:T(8,128)(2,1)S(1)} fusion(pred[256,64]{0,1:T(8,128)(4,1)S(1)} %iota_compare_fusion, pred[16,256]{1,0:T(8,128)(4,1)S(1)} %iota_compare_fusion.1, bf16[2,16,1,256,512]{4,3,2,1,0:T(8,128)(2,1)} %param.6), kind=kOutput, calls=%fused_computation.6 | convolution fusion | flops 538181632 | bytes 10506240 | tf_op jit(solution)/shard_map/rpsn,psa->rpan/dot_general | solution.py:237
  6.3 2.1 %reshape.318 = bf16[2,16,64,4,128]{4,3,2,0,1:T(4,128)(2,1)} reshape(bf16[2,16,64,512]{3,2,0,1:T(8,128)(2,1)S(1)} %convert_bitcast_fusion.1) | data formatting | bytes 4194304 | tf_op jit(solution)/shard_map/reshape | solution.py:238
  8.4 6.3 %convert_bitcast_fusion = bf16[16,2,64,4,128]{4,0,1,3,2:T(8,128)(2,1)S(1)} fusion(bf16[64,4,128,128]{3,2,1,0:T(8,128)(2,1)} %param.10, bf16[2,16,64,4,128]{4,3,2,0,1:T(4,128)(2,1)} %reshape.318), kind=kOutput, calls=%fused_computation.5 | convolution fusion | flops 269484032 | bytes 12582912 | tf_op jit(solution)/shard_map/rpagj,agjt->pragt/dot_general | solution.py:239
  14.7 0.0 copy-start
  14.7 2.4 %copy.12 = bf16[16,2,64,4,128]{4,3,2,1,0:T(4,128)(2,1)} copy(bf16[16,2,64,4,128]{4,0,1,3,2:T(8,128)(2,1)S(1)} %convert_bitcast_fusion) | data formatting | bytes 4194304 | tf_op jit(solution)/shard_map/convert_element_type | solution.py:239
  17.1 0.0 copy-done
  17.1 0.1 copy.13
  17.2 0.1 reshape.320
  17.3 1.1 sine_multiply_fusion.1
  18.4 0.1 multiply_convert_fusion
  18.5 1.1 maximum_maximum_fusion.refs_1_
  19.6 1.1 negate_convert_fusion
  20.7 1.0 fusion.28
  21.7 0.8 maximum_maximum_fusion.1.refs_2_
  22.5 0.1 cosine_multiply_fusion.1
  22.6 0.6 pad_maximum_fusion.refs_4_
  23.2 95.6 %combine.1 = f32[2,16,32,256]{3,2,1,0:T(8,128)} custom-call(bf16[16,512,128]{2,1,0:T(8,128)(2,1)} %bitcast.26, bf16[2,512,512]{2,1,0:T(8,128)(2,1)} %maximum_maximum_fusion.refs_1_, bf16[512,512]{1,0:T(8,128)(2,1)} %maximum_maximum_fusion.1.refs_2_, bf16[2,256,256]{2,1,0:T(8,128)(2,1)} %bitcast.27, f32[2,16,16]{2,1,0:T(8,128)} %pad_maximum_fusion.refs_4_), custom_call_target="tpu_custom_call" | custom-call | tf_op jit(solution)/shard_map/combine/pallas_call | solution.py:271
  118.8 2.3 %copy.25 = f32[2,16,32,256]{3,2,1,0:T(8,128)} copy(f32[2,16,32,256]{3,2,1,0:T(8,128)} %combine.1) | data formatting | bytes 2097152
  (3 shorter events, 0.0 us)
Async XLA Ops:
  14.7 2.4 %copy-start = (s32[64,4]{0,1:T(4,128)S(1)}, s32[64,4]{0,1:T(4,128)}, u32[]{:S(2)}) copy-start(s32[64,4]{0,1:T(4,128)} %param.9) | copy-start | bytes 3076

commit v2 on v1

v2 whole, which is shorter than its diff:
```python
import functools
import math

import jax
import jax.numpy as jnp
from jax import lax
from jax.experimental import pallas as pl
from jax.experimental.pallas import tpu as pltpu
from jax.sharding import PartitionSpec as P

F32 = jnp.float32
BF16 = jnp.bfloat16
SUB = 2
SUBLANE, LANE = 8, 128


def cos_sin(product, length, dtype):
    phase = (product % length).astype(F32) * (2.0 * jnp.pi / length)
    scale = 1.0 / jnp.sqrt(F32(length))
    return ((jnp.cos(phase) * scale).astype(dtype), (jnp.sin(phase) * scale).astype(dtype))


def halving_orders(bits):
    first = list(range(bits))
    return [first, first[:1] + first[:0:-1]]


def kernel(bits, groups, parts, rows, side, *refs):
    contrib, ymat, xmat, sens, twiddle, out = refs[:6]
    weighted, raw, part_out, part_in = refs[6:10]
    inbox = refs[10 : 10 + bits]
    first_send, first_recv, half_send, half_recv, line_send, line_recv = refs[10 + bits :]
    blocks = 1 << bits
    orders = halving_orders(bits)
    lanes = side // LANE
    steps = rows // SUBLANE
    coil = lax.axis_index("coil")
    kz = lax.axis_index("kz")
    my_bit = [(coil // (1 << bit)) % 2 for bit in range(bits)]
    partner = [coil + (1 - 2 * my_bit[bit]) * (1 << bit) for bit in range(bits)]
    last = groups - 1
    inner = (kz > 0) & (kz < last)
    outer = (kz == 0) | (kz == last)
    inward = jnp.where(kz < 2, kz + 1, kz - 1)
    outward = jnp.where(kz < 2, 0, last)
    far_end = last - outward

    barrier = pltpu.get_barrier_semaphore()
    for bit in range(bits):
        pl.semaphore_signal(barrier, 1, device_id={"coil": partner[bit]})
    pl.semaphore_signal(barrier, 1, device_id={"kz": (kz + 1) % groups})
    pl.semaphore_signal(barrier, 1, device_id={"kz": (kz + groups - 1) % groups})
    pl.semaphore_wait(barrier, bits + 2)

    def kept_start(order, stage):
        start = 0
        for s in range(stage):
            start = start + my_bit[order[s]] * (blocks >> (s + 1))
        return start

    half = blocks // 2

    def first_copy(pair):
        span = pl.ds(pair * SUB, SUB)
        return pltpu.make_async_remote_copy(
            src_ref=weighted.at[:, pl.ds((1 - my_bit[0]) * half, half), span],
            dst_ref=inbox[0].at[:, :, span],
            send_sem=first_send.at[pair],
            recv_sem=first_recv.at[pair],
            device_id={"coil": partner[0]},
        )

    def half_copy(chunk, lane, stage):
        order = orders[lane % 2]
        bit = order[stage]
        size = blocks >> (stage + 1)
        start = kept_start(order, stage) + (1 - my_bit[bit]) * size
        return pltpu.make_async_remote_copy(
            src_ref=weighted.at[chunk, pl.ds(start, size)],
            dst_ref=inbox[stage].at[chunk],
            send_sem=half_send.at[stage - 1, chunk],
            recv_sem=half_recv.at[stage - 1, chunk],
            device_id={"coil": partner[bit]},
        )

    def add_inbox(chunk, lane, stage):
        size = blocks >> (stage + 1)
        start = kept_start(orders[lane % 2], stage + 1)
        for b in range(size):
            total = weighted[chunk, start + b] + inbox[stage][chunk, b]
            if stage < bits - 1:
                weighted[chunk, start + b] = total
            else:
                raw[chunk, kz] = total

    def line_copy(kind, chunk, src, dst, to):
        return pltpu.make_async_remote_copy(
            src_ref=src,
            dst_ref=dst,
            send_sem=line_send.at[kind, chunk],
            recv_sem=line_recv.at[kind, chunk],
            device_id={"kz": to},
        )

    def from_outer(chunk, source):
        return line_copy(0, chunk, raw.at[chunk, source], raw.at[chunk, source], inward)

    def from_inner(chunk, source):
        return line_copy(1, chunk, raw.at[chunk, source], raw.at[chunk, source], inward)

    def forward(chunk, source):
        return line_copy(2, chunk, raw.at[chunk, source], raw.at[chunk, source], inward)

    def partial(chunk):
        return line_copy(3, chunk, part_out.at[chunk], part_in.at[chunk], outward)

    def compute(pair):
        first = pair * SUB
        data = jnp.concatenate([contrib[first + s] for s in range(SUB)], axis=1)
        seg = data.shape[1] // SUB
        halves = [
            jnp.dot(ymat[h], data, preferred_element_type=F32).astype(BF16)
            for h in range(side // seg)
        ]
        s_re = sens[0].astype(F32)
        s_im = sens[1].astype(F32)
        for s in range(SUB):
            pieces = [h[r * side : (r + 1) * side, s * seg : (s + 1) * seg] for r in range(2) for h in halves]
            image = jnp.dot(jnp.concatenate(pieces, axis=1), xmat[...], preferred_element_type=F32)
            i_re, i_im = image[:, :side], image[:, side:]
            result = [s_re * i_re + s_im * i_im, s_re * i_im - s_im * i_re]
            for block in range(blocks):
                for lane in range(lanes):
                    place = 0
                    for bit in orders[lane % 2]:
                        place = place * 2 + (block >> bit) % 2
                    for step in range(steps):
                        top = block * rows + step * SUBLANE
                        for r in range(2):
                            weighted[step * lanes + lane, place, first + s, r] = result[r][
                                top : top + SUBLANE, lane * LANE : (lane + 1) * LANE
                            ]

    def transform(chunk, sources, table, store):
        for q in range(groups):
            sums = []
            for k in range(parts):
                re = im = None
                for j in sources:
                    angle = 2.0 * math.pi * (q * j % groups) / groups
                    c, d = round(math.cos(angle), 12), round(math.sin(angle), 12)
                    x_re, x_im = raw[chunk, j, k, 0], raw[chunk, j, k, 1]
                    for coef, a, b in ((c, x_re, x_im), (d, x_im, -x_re)):
                        if coef == 0.0:
                            continue
                        ta = a if coef == 1.0 else a * F32(coef)
                        tb = b if coef == 1.0 else b * F32(coef)
                        re = ta if re is None else re + ta
                        im = tb if im is None else im + tb
                sums.append((re, im))
            for z in range(q, parts, groups):
                a_re = a_im = None
                for k in range(parts):
                    c, d = twiddle[2 * table, k, z], twiddle[2 * table + 1, k, z]
                    re, im = sums[k]
                    t_re, t_im = c * re + d * im, c * im - d * re
                    a_re = t_re if a_re is None else a_re + t_re
                    a_im = t_im if a_im is None else a_im + t_im
                store(z, a_re, a_im)

    def spot(step, lane):
        return pl.ds(pl.multiple_of(step * SUBLANE, SUBLANE), SUBLANE), pl.ds(lane * LANE, LANE)

    def into_out(step, lane):
        y, x = spot(step, lane)

        def store(z, re, im):
            out[0, z, y, x] = re
            out[1, z, y, x] = im

        return store

    def into_partial(chunk):
        def store(z, re, im):
            part_out[chunk, z, 0] = re
            part_out[chunk, z, 1] = im

        return store

    def each_pair(pair, carry):
        compute(pair)
        first_copy(pair).start()
        return carry

    pairs = parts // SUB
    lax.fori_loop(0, pairs, each_pair, 0)

    def first_wait(pair, carry):
        first_copy(pair).wait_recv()
        return carry

    lax.fori_loop(0, pairs, first_wait, 0)

    def reduce_stage(stage, step):
        for lane in range(lanes):
            chunk = step * lanes + lane
            if stage:
                half_copy(chunk, lane, stage).wait_recv()
            add_inbox(chunk, lane, stage)
            if stage < bits - 1:
                half_copy(chunk, lane, stage + 1).start()
            else:

                @pl.when(outer)
                def _():
                    from_outer(chunk, kz).start()

                @pl.when(inner)
                def _():
                    from_inner(chunk, kz).start()

    def relay_stage(step):
        for lane in range(lanes):
            chunk = step * lanes + lane

            @pl.when(inner)
            def _():
                from_outer(chunk, outward).wait_recv()
                forward(chunk, outward).start()

            for end in (0, last):

                @pl.when(kz == end)
                def _(end=end):
                    transform(chunk, [end], 0, into_out(step, lane))

    def combine_stage(step):
        for lane in range(lanes):
            chunk = step * lanes + lane

            @pl.when(inner)
            def _():
                from_inner(chunk, inward).wait_recv()
                forward(chunk, far_end).wait_recv()

            for place, end in ((1, 0), (last - 1, last)):

                @pl.when(kz == place)
                def _(end=end):
                    transform(chunk, [j for j in range(groups) if j != end], 1, into_partial(chunk))
                    partial(chunk).start()

            @pl.when(inner)
            def _():
                transform(chunk, list(range(groups)), 0, into_out(step, lane))

    def finish_stage(step):
        for lane in range(lanes):
            chunk = step * lanes + lane

            @pl.when(outer)
            def _():
                partial(chunk).wait_recv()
                y, x = spot(step, lane)
                for r in range(2):
                    out[r, :, y, x] = out[r, :, y, x] + part_in[chunk, :, r]

    def tick(t, carry):
        def at(lag, body):
            step = t - lag

            @pl.when((step >= 0) & (step < steps))
            def _():
                body(step)

        at(bits, relay_stage)
        for stage in range(bits - 1, -1, -1):
            at(stage, functools.partial(reduce_stage, stage))
        at(bits + 1, combine_stage)
        at(bits + 2, finish_stage)
        return carry

    lax.fori_loop(0, steps + bits + 2, tick, 0)

    def drain_first(pair, carry):
        first_copy(pair).wait_send()
        return carry

    lax.fori_loop(0, pairs, drain_first, 0)

    def drain(step, carry):
        for lane in range(lanes):
            chunk = step * lanes + lane
            for stage in range(1, bits):
                half_copy(chunk, lane, stage).wait_send()

            @pl.when(outer)
            def _():
                from_outer(chunk, kz).wait_send()

            @pl.when(inner)
            def _():
                from_inner(chunk, kz).wait_send()
                forward(chunk, outward).wait_send()
                partial(chunk).wait_send()

        return carry

    lax.fori_loop(0, steps, drain, 0)


def per_device(kdata, spoke_angle, spoke_count, block_index, interp, sens_maps):
    side = sens_maps.shape[2]
    parts = kdata.shape[1]
    spokes = kdata.shape[3]
    angles, segs, seg = interp.shape[:3]
    coils = lax.axis_size("coil")
    groups = lax.axis_size("kz")
    bits = coils.bit_length() - 1
    rows = side // coils
    length = parts * groups
    kz = lax.axis_index("kz")

    position = jnp.arange(spokes, dtype=jnp.int32)
    used = position[None, :] < spoke_count[:, None]
    match = spoke_angle[:, None] == jnp.arange(angles, dtype=jnp.int32)[None, :]
    weights = (used[:, :, None] & match[None, :, :]).astype(BF16)
    binned = jnp.einsum("rpsn,psa->rpan", kdata[:, :, 0], weights, preferred_element_type=F32).astype(BF16)
    pieces = binned.reshape(2, parts, angles, segs, seg)
    contrib = jnp.einsum("rpagj,agjt->pragt", pieces, interp, preferred_element_type=F32).astype(BF16)
    hits = angles * segs
    contrib = contrib.reshape(parts, 2 * hits, seg)

    across = side // seg
    index = jnp.arange(side, dtype=jnp.int32)
    where = block_index.reshape(-1)
    hit_y = where // across
    hit_x = where % across
    cos_y, sin_y = cos_sin(index[:, None] * hit_y[None, :], side, F32)
    here = (jnp.arange(across, dtype=jnp.int32)[:, None, None] == hit_x).astype(F32)
    cos_y, sin_y = cos_y * here, sin_y * here
    ymat = jnp.concatenate(
        [jnp.concatenate([cos_y, sin_y], 2), jnp.concatenate([-sin_y, cos_y], 2)], 1
    ).astype(BF16)
    cos_x, sin_x = cos_sin(index[:, None] * index[None, :], side, F32)
    xmat = jnp.concatenate(
        [jnp.concatenate([cos_x, -sin_x], 1), jnp.concatenate([sin_x, cos_x], 1)], 0
    ).astype(BF16)
    low = jnp.arange(parts, dtype=jnp.int32)
    outward = jnp.where(kz < 2, 0, groups - 1)
    tables = []
    for owner in (kz, outward):
        tables += cos_sin(low[:, None] * (owner * parts + low)[None, :], length, F32)
    twiddle = jnp.stack(tables)

    assert groups == 4 and parts % groups == 0
    chunks = (rows // SUBLANE) * (side // LANE)
    block = (parts, 2, SUBLANE, LANE)
    vmem = pl.BlockSpec(memory_space=pltpu.VMEM)
    scratch = [
        pltpu.VMEM((chunks, coils) + block, F32),
        pltpu.VMEM((chunks, groups) + block, F32),
        pltpu.VMEM((chunks,) + block, F32),
        pltpu.VMEM((chunks,) + block, F32),
    ]
    scratch += [pltpu.VMEM((chunks, coils >> (s + 1)) + block, F32) for s in range(bits)]
    scratch += [pltpu.SemaphoreType.DMA((parts // SUB,))] * 2
    scratch += [pltpu.SemaphoreType.DMA((bits - 1, chunks))] * 2
    scratch += [pltpu.SemaphoreType.DMA((4, chunks))] * 2
    return pl.pallas_call(
        functools.partial(kernel, bits, groups, parts, rows, side),
        out_shape=jax.ShapeDtypeStruct((2, parts, rows, side), F32),
        in_specs=[vmem] * 4 + [pl.BlockSpec(memory_space=pltpu.SMEM)],
        out_specs=vmem,
        scratch_shapes=scratch,
        compiler_params=pltpu.CompilerParams(
            collective_id=0, has_side_effects=True, vmem_limit_bytes=60 * 1024 * 1024
        ),
        name="combine",
    )(contrib, ymat, xmat, sens_maps[:, 0], twiddle)


def solution(mesh):
    placed = (
        P(None, "kz", "coil", None, None),
        P(),
        P("kz"),
        P(),
        P(),
        P(None, "coil", None, None),
    )
    return jax.shard_map(
        per_device,
        mesh=mesh,
        in_specs=placed,
        out_specs=P(None, "kz", "coil", None),
        check_vma=False,
    )
```

time: 121 us -> 107 us (0.88)
  Pallas kernels: 95.6 us -> 81.2 us
    pallas_call x1, Pallas kernels: 95.6 us -> 81.2 us  [per_device(): pl.pallas_call(functools.partial(kernel, bits, groups, parts, rows, side)...]
where the time goes in v2:
time: 107 us
  Pallas kernels  81.2 us (76%)
  matrix products  11.2 us (10%)
  other arithmetic  7.27 us (7%)
  local copies, waits for them, and re-layouts  7.02 us (7%)
    pallas_call x1, Pallas kernels, per_device(): pl.pallas_call(functools.partial(kernel, bits, groups, parts, rows, side)...  81.2 us
    dot_general x1, matrix products, per_device(): jnp.einsum('rpagj,agjt->pragt', pieces, interp, preferred_element_type=F32)  6.31 us
    dot_general x1, matrix products, per_device(): jnp.einsum('rpsn,psa->rpan', kdata[:, :, 0], weights, preferred_element_t...  4.86 us
    convert_element_type x1, local copies, waits for them, and re-layouts, per_device(): jnp.einsum('rpagj,agjt->pragt', pieces, interp, preferred_element_type=F32)  2.43 us
    unnamed x4, local copies, waits for them, and re-layouts  2.41 us
    another operation x3, other arithmetic  2.19 us

profile of v2, /device:TPU:0, one launch (start us, length us, event | category | flops | bytes accessed | tf_op | source)
XLA Modules:
  0.0 106.8 jit_solution(12699333527203740106)
XLA Ops:
  0.0 0.7 iota_compare_fusion
  0.7 0.7 iota_compare_fusion.1
  1.4 4.9 %convert_bitcast_fusion.1 = bf16[2,16,64,512]{3,2,0,1:T(8,128)(2,1)S(1)} fusion(pred[256,64]{0,1:T(8,128)(4,1)S(1)} %iota_compare_fusion, pred[16,256]{1,0:T(8,128)(4,1)S(1)} %iota_compare_fusion.1, bf16[2,16,1,256,512]{4,3,2,1,0:T(8,128)(2,1)} %param.6), kind=kOutput, calls=%fused_computation.6 | convolution fusion | flops 538181632 | bytes 10506240 | tf_op jit(solution)/shard_map/rpsn,psa->rpan/dot_general | solution.py:328
  6.3 2.1 %reshape.394 = bf16[2,16,64,4,128]{4,3,2,0,1:T(4,128)(2,1)} reshape(bf16[2,16,64,512]{3,2,0,1:T(8,128)(2,1)S(1)} %convert_bitcast_fusion.1) | data formatting | bytes 4194304 | tf_op jit(solution)/shard_map/reshape | solution.py:329
  8.4 6.3 %convert_bitcast_fusion = bf16[16,2,64,4,128]{4,0,1,3,2:T(8,128)(2,1)S(1)} fusion(bf16[64,4,128,128]{3,2,1,0:T(8,128)(2,1)} %param.10, bf16[2,16,64,4,128]{4,3,2,0,1:T(4,128)(2,1)} %reshape.394), kind=kOutput, calls=%fused_computation.5 | convolution fusion | flops 269484032 | bytes 12582912 | tf_op jit(solution)/shard_map/rpagj,agjt->pragt/dot_general | solution.py:330
  14.7 0.0 copy-start
  14.7 2.4 %copy.12 = bf16[16,2,64,4,128]{4,3,2,1,0:T(4,128)(2,1)} copy(bf16[16,2,64,4,128]{4,0,1,3,2:T(8,128)(2,1)S(1)} %convert_bitcast_fusion) | data formatting | bytes 4194304 | tf_op jit(solution)/shard_map/convert_element_type | solution.py:330
  17.1 0.0 copy-done
  17.1 0.1 copy.13
  17.2 0.1 reshape.396
  17.3 1.1 sine_multiply_fusion.1
  18.4 0.1 multiply_convert_fusion
  18.5 1.1 maximum_maximum_fusion.refs_1_
  19.6 1.1 %negate_convert_fusion = (bf16[256,256]{1,0:T(8,128)(2,1)S(1)}, bf16[256,256]{1,0:T(8,128)(2,1)S(1)}) fusion(), kind=kLoop, calls=%fused_computation.29 | loop fusion | flops 1245184 | bytes 262144 | tf_op jit(solution)/shard_map/convert.5
  20.7 1.0 fusion.28
  21.7 0.8 maximum_maximum_fusion.1.refs_2_
  22.5 0.1 cosine_multiply_fusion.1
  22.6 0.6 pad_maximum_fusion.refs_4_
  23.2 81.2 %combine.1 = f32[2,16,32,256]{3,2,1,0:T(8,128)} custom-call(bf16[16,512,128]{2,1,0:T(8,128)(2,1)} %bitcast.26, bf16[2,512,512]{2,1,0:T(8,128)(2,1)} %maximum_maximum_fusion.refs_1_, bf16[512,512]{1,0:T(8,128)(2,1)} %maximum_maximum_fusion.1.refs_2_, bf16[2,256,256]{2,1,0:T(8,128)(2,1)} %bitcast.27, f32[4,16,16]{2,1,0:T(8,128)} %pad_maximum_fusion.refs_4_), custom_call_target="tpu_custom_call" | custom-call | tf_op jit(solution)/shard_map/combine/pallas_call | solution.py:370
  104.5 2.3 %copy.25 = f32[2,16,32,256]{3,2,1,0:T(8,128)} copy(f32[2,16,32,256]{3,2,1,0:T(8,128)} %combine.1) | data formatting | bytes 2097152
  (4 shorter events, 0.0 us)
Async XLA Ops:
  14.7 2.4 %copy-start = (s32[64,4]{0,1:T(4,128)S(1)}, s32[64,4]{0,1:T(4,128)}, u32[]{:S(2)}) copy-start(s32[64,4]{0,1:T(4,128)} %param.9) | copy-start | bytes 3076
